TPU v7x, 256 devices: a whole 4x4x8 slice. The times are simulated.
256 devices in a mesh: gx: 4 (over z_lo), gy: 8 (over x, z_hi), gz: 8 (over y, core).
Axes of the slice: x: 4, y: 4, z: 8 (z_hi: 2, z_lo: 4; z = z_hi * 4 + z_lo), core: 2. Of those that a mesh axis runs over, the one named last changes fastest.
Arguments:
- attn_out: bfloat16 [16384, 8192], P('gx', ('gy', 'gz')), may hold values from -16 to 16
- out_grad: bfloat16 [16384, 8192], P('gx', ('gz', 'gy')), may hold values from -0.046875 to 0.046875
- valid_counts: int32 [16], P('gx'), may hold values from 128 to 1024
Outputs:
- weight_grad: float32 [8192, 8192], P(('gy', 'gx'), 'gz')
Inputs may be any that keep to these rules, and one draw needn't show every extreme that they name: `valid_counts`: valid tokens of a packed row come first, padding after.
All inputs are finite; a program needn't handle non-finite values.
Results may differ from a plain program's by a relative error of at most 0.0003.
Values may be sent and summed in bfloat16 or wider, within the bound.
A program may use at most 64 MiB of HBM per device.

v0:
```python
import jax
import jax.numpy as jnp
from jax import lax
from jax.sharding import Mesh
from jax.sharding import PartitionSpec as P

GY = ("gy_0", "gy_1")
GY_GZ = ("gy_0", "gy_1", "gz")
GZ_GY = ("gz", "gy_0", "gy_1")
GY_GX = ("gy_0", "gy_1", "gx")


def whole_of(value, axes, dim):
    out = value
    for number in range(len(axes) - 1, -1, -1):
        out = lax.all_gather(out, axes[number], axis=dim, tiled=True)
    return out


def split_up(value, dim, peers):
    lengths = value.shape
    tiles = value.reshape(*lengths[:dim], peers, lengths[dim] // peers, *lengths[dim + 1 :])
    return jnp.moveaxis(tiles, dim, 0)


def summed_on_arrival(value, axis, dim):
    tiles = split_up(value, dim, lax.axis_size(axis))
    arrived = lax.all_to_all(tiles, axis, split_axis=0, concat_axis=0, tiled=True)
    return arrived.sum(axis=0)


def transpose_product(inputs, grads):
    return lax.dot_general(
        inputs, grads, (((0,), (0,)), ((), ())), preferred_element_type=jnp.float32
    )


def shards(attn_out, out_grad, valid_counts):
    rows_here = valid_counts.shape[0]
    slot_count = attn_out.shape[0] // rows_here
    positions = lax.broadcasted_iota(jnp.int32, (rows_here, slot_count), 1)
    kept_rows = (positions < valid_counts[:, None]).reshape(-1)
    gathered_inputs = lax.all_gather(attn_out, "gz", axis=1, tiled=True)
    gathered_grads = whole_of(out_grad, GY, 1)
    masked = jnp.where(kept_rows[:, None], gathered_grads, jnp.zeros((), gathered_grads.dtype))
    partial_grad = transpose_product(gathered_inputs, masked)
    return summed_on_arrival(partial_grad, "gx", 0)


def solution(mesh):
    split = Mesh(
        mesh.devices.reshape(mesh.shape["gx"], 4, 2, mesh.shape["gz"]), ("gx", "gy_0", "gy_1", "gz")
    )
    return jax.shard_map(
        shards,
        mesh=split,
        in_specs=(P("gx", GY_GZ), P("gx", GZ_GY), P("gx")),
        out_specs=P(GY_GX, "gz"),
        check_vma=False,
    )
```

profile of v0, /device:TPU:8, one launch (start us, length us, event | category | flops | bytes accessed | tf_op | source)
XLA Modules:
  0.0 345.3 jit_solution(17290514149555261762)
XLA Ops:
  6.5 0.0 all-gather.4.cloned.1.call-start
  6.5 0.7 all-gather.4.cloned.1.call-update
  7.3 0.0 all-gather.8.cloned.1.call-start
  7.3 0.7 all-gather.8.cloned.1.call-update
  8.0 0.0 all-gather.6.cloned.1.call-start
  8.1 69.1 %all-gather.4.cloned.1.call-done = bf16[4096,256]{1,0:T(8,128)(2,1)} async-done(((bf16[4096,128]{1,0:T(8,128)(2,1)}), bf16[4096,256]{1,0:T(8,128)(2,1)}) %all-gather.4.cloned.1.call-update) | async-done | bytes 2097168 | tf_op jit(solution)/shard_map/all_gather | solution.py:16
  77.1 0.0 all-gather.6.cloned.1.call-update
  77.2 0.7 fusion.4
  77.9 53.2 %all-gather.8.cloned.1.call-done = bf16[4096,1024]{1,0:T(8,128)(2,1)} async-done(((bf16[4096,128]{1,0:T(8,128)(2,1)}), bf16[4096,1024]{1,0:T(8,128)(2,1)}) %all-gather.8.cloned.1.call-update) | async-done | bytes 8388624 | tf_op jit(solution)/shard_map/all_gather | solution.py:43
  131.1 92.2 %all-gather.6.cloned.1.call-done = bf16[4096,1024]{1,0:T(8,128)(2,1)} async-done(((bf16[4096,256]{1,0:T(8,128)(2,1)}), bf16[4096,1024]{1,0:T(8,128)(2,1)}) %all-gather.6.cloned.1.call-update) | async-done | bytes 8388624 | tf_op jit(solution)/shard_map/all_gather | solution.py:16
  223.3 15.3 %fusion = f32[1024,1024]{0,1:T(8,128)S(1)} fusion(bf16[4096,1024]{1,0:T(8,128)(2,1)} %all-gather.8.cloned.1.call-done, bf16[4096,1024]{1,0:T(8,128)(2,1)} %all-gather.6.cloned.1.call-done, pred[4096]{0:T(1024)(128)(4,1)S(1)} %bitcast.10), kind=kOutput, calls=%fused_computation | convolution fusion | flops 8594128896 | bytes 20975616 | tf_op jit(solution)/shard_map/dot_general | solution.py:33
  238.6 96.5 %all_to_all.5 = f32[4,256,1024]{2,1,0:T(8,128)} all-to-all(f32[4,256,1024]{2,1,0:T(8,128)S(1)} %bitcast.9), channel_id=1, replica_groups=mesh['gx'=4,'gy_0'=4,'gy_1'=2,'gz'=8] {'gx'}, dimensions={0} | all-to-all | bytes 8388608 | tf_op jit(solution)/shard_map/all_to_all | solution.py:28
  335.1 3.7 %reduce_sum.9 = f32[256,1024]{1,0:T(8,128)} reduce(f32[4,256,1024]{2,1,0:T(8,128)} %all_to_all.5, f32[]{:T(128)} %constant.1.clone.1), dimensions={0}, to_apply=%region_0.1 | reduce | flops 786432 | bytes 5242884 | tf_op jit(solution)/shard_map/reduce_sum | solution.py:29
  (1 shorter events, 0.0 us)
Async XLA Ops:
  6.5 70.6 %all-gather.4.cloned.1.call-start = ((), (), s32[]{:S(2)}) async-start(), calls=%async_computation.1 | async-start | bytes 3145728 | tf_op jit(solution)/shard_map/all_gather | solution.py:16
  7.3 123.8 %all-gather.8.cloned.1.call-start = ((), (), s32[]{:S(2)}) async-start(), calls=%async_computation.3 | async-start | bytes 9437184 | tf_op jit(solution)/shard_map/all_gather | solution.py:43
  8.0 215.3 %all-gather.6.cloned.1.call-start = ((), (), s32[]{:S(2)}) async-start(), calls=%async_computation.2 | async-start | bytes 10485760 | tf_op jit(solution)/shard_map/all_gather | solution.py:16
Sparse Core Ops, SparseCore 0:
  9.1 67.9 all-gather.3
  79.0 52.0 all-gather.7
  132.9 90.3 all-gather.5
where the time goes:
time: 345 us
  waiting for transfers between devices  216 us (63%)
  blocking collectives  96.5 us (28%)
  matrix products  15.3 us (4%)
  between operations  13.1 us (4%)
  other arithmetic  4.42 us (1%)
    all_gather x2, waiting for transfers between devices, whole_of(): out = lax.all_gather(out, axes[number], axis=dim, tiled=True)  161 us
    all_to_all x1, blocking collectives, summed_on_arrival(): lax.all_to_all(tiles, axis, split_axis=0, concat_axis=0, tiled=True)  96.5 us
    all_gather x1, waiting for transfers between devices, shards(): gathered_inputs = lax.all_gather(attn_out, 'gz', axis=1, tiled=True)  53.2 us
    dot_general x1, matrix products, transpose_product(): lax.dot_general(inputs, grads, (((0,), (0,)), ((), ())), preferred_elemen...  15.3 us
  transfers between devices with their start and end apart: 3, of which 3 were waited for; matrix products, arithmetic and copies ran while one was open for 0% of the time, Pallas kernels for 0%

commit v1 on v0

v1 whole, which is shorter than its diff:
```python
import functools

import jax
import jax.numpy as jnp
from jax import lax
from jax.experimental import pallas as pl
from jax.experimental.pallas import tpu as pltpu
from jax.sharding import PartitionSpec as P

MESH = pl.DeviceIdType.MESH
TOK = 4096
SEQ = 1024
BLK = 128
CHK = TOK // 4
HALF = TOK // 2
COPIES = 64


def kernel(vc, a_hbm, b_hbm, out, raw, at, bb, sbuf, rbuf, ssc, rsc, lsem, ss, rs):
    zl = lax.axis_index("gx")
    gy = lax.axis_index("gy")
    gz = lax.axis_index("gz")
    x, zh = gy // 2, gy % 2
    y, c = gz // 2, gz % 2
    xr, xl, xo = (x + 1) % 4, (x + 3) % 4, (x + 2) % 4
    yr, yl, yo = (y + 1) % 4, (y + 3) % 4, (y + 2) % 4

    right, left = (zl, xr * 2 + zh, gz), (zl, xl * 2 + zh, gz)
    far = (zl, x * 2 + (1 - zh), gz)
    up, down = (zl, gy, yr * 2 + c), (zl, gy, yl * 2 + c)
    opposite = (zl, gy, yo * 2 + c)
    sibling = (zl, gy, y * 2 + (1 - c))
    owners = [((zl + d) % 4, gy, gz) for d in range(1, 4)]

    barrier = pltpu.get_barrier_semaphore()
    partners = [right, left, far, up, down, sibling] + owners
    for dev in partners:
        pl.semaphore_signal(barrier, inc=1, device_id=dev, device_id_type=MESH)

    load_a = pltpu.make_async_copy(a_hbm, raw, lsem.at[0])
    load_b = pltpu.make_async_copy(b_hbm, bb.at[gy], lsem.at[1])
    load_a.start()
    load_b.start()
    pl.semaphore_wait(barrier, len(partners))

    made = []

    def remote(src, dst, dev):
        k = len(made)
        copy = pltpu.make_async_remote_copy(
            src_ref=src,
            dst_ref=dst,
            send_sem=ss.at[k],
            recv_sem=rs.at[k],
            device_id=dev,
            device_id_type=MESH,
        )
        made.append(copy)
        return copy

    def tokens(q, size):
        return pl.ds(q * size, size)

    far_q = {q: remote(b_hbm.at[tokens(q, CHK)], bb.at[gy, tokens(q, CHK)], far) for q in range(4)}
    own_r = {h: remote(b_hbm.at[tokens(h, HALF)], bb.at[gy, tokens(h, HALF)], right) for h in range(2)}
    own_l = {h: remote(b_hbm.at[tokens(h, HALF)], bb.at[gy, tokens(h, HALF)], left) for h in range(2)}

    def relay(slot, q, size, dev):
        return remote(bb.at[slot, tokens(q, size)], bb.at[slot, tokens(q, size)], dev)

    hop_r = relay(xl * 2 + zh, 0, HALF, right)
    hop_l = relay(xr * 2 + zh, 1, HALF, left)
    oz = 1 - zh
    far_r = {q: relay(x * 2 + oz, q, CHK, right) for q in range(4)}
    far_l = {q: relay(x * 2 + oz, q, CHK, left) for q in range(4)}
    fhop_r = {q: relay(xl * 2 + oz, q, CHK, right) for q in (0, 1)}
    fhop_l = {q: relay(xr * 2 + oz, q, CHK, left) for q in (2, 3)}

    def rows(block, h=None):
        if h is None:
            return pl.ds(pl.multiple_of(block * BLK, BLK), BLK)
        return pl.ds(pl.multiple_of(block * BLK + h * (BLK // 2), BLK // 2), BLK // 2)

    def pass_on(block, h, dev):
        return remote(at.at[rows(block, h)], at.at[rows(block, h)], dev)

    a_up = {h: pass_on(gz, h, up) for h in range(2)}
    a_down = {h: pass_on(gz, h, down) for h in range(2)}
    ahop_up = pass_on(yl * 2 + c, 0, up)
    ahop_down = pass_on(yr * 2 + c, 1, down)
    sib = {d: pass_on(((y + d) % 4) * 2 + c, None, sibling) for d in range(4)}

    for q in (0, 2, 1, 3):
        far_q[q].start()
    own_r[0].start()
    own_l[1].start()
    own_r[1].start()
    own_l[0].start()

    load_a.wait()

    def turn(k, carry):
        lanes = lax.broadcasted_iota(jnp.int32, (BLK, BLK), 1) + (k % (SEQ // BLK)) * BLK
        kept = lanes < vc[k // (SEQ // BLK)]
        span = pl.ds(pl.multiple_of(k * BLK, BLK), BLK)
        tile = raw[span, :].T
        at[rows(gz), span] = jnp.where(kept, tile, jnp.zeros((), tile.dtype))
        return carry

    lax.fori_loop(0, TOK // BLK, turn, 0)
    a_up[0].start()
    a_down[1].start()
    a_up[1].start()
    a_down[0].start()
    sib[0].start()

    own_r[0].wait_recv()
    hop_r.start()
    own_l[1].wait_recv()
    hop_l.start()
    far_q[0].wait_recv()
    far_r[0].start()
    far_l[0].start()
    a_up[0].wait_recv()
    ahop_up.start()
    a_down[1].wait_recv()
    ahop_down.start()
    far_q[2].wait_recv()
    far_r[2].start()
    far_l[2].start()
    a_up[1].wait_recv()
    sib[3].start()
    a_down[0].wait_recv()
    sib[1].start()
    far_q[1].wait_recv()
    far_r[1].start()
    far_l[1].start()
    ahop_up.wait_recv()
    ahop_down.wait_recv()
    sib[2].start()
    for d in range(4):
        sib[d].wait_recv()

    sends = {}
    for n in range(4):
        for d in range(3):
            sends[n, d] = (
                remote(sbuf.at[d, n], rbuf.at[d, n], owners[d]),
                remote(ssc.at[d, n], rsc.at[d, n], owners[d]),
            )

    def columns(slot):
        return pl.ds(pl.multiple_of(slot * BLK, BLK), BLK)

    def product(d, first, second):
        lhs = at[pl.ds(pl.multiple_of(((zl + d) % 4) * 2 * BLK, 2 * BLK), 2 * BLK), :]
        rhs = jnp.concatenate([bb[first], bb[second]], axis=1)
        return jnp.dot(lhs, rhs, preferred_element_type=jnp.float32)

    def pair(n, first, second):
        for d in range(3):
            part = product(d + 1, first, second)
            top = jnp.maximum(jnp.max(jnp.abs(part), axis=0, keepdims=True), 2e-34)
            sbuf[d, n] = jnp.round(part * (32767.0 / top)).astype(jnp.int32).astype(jnp.int16)
            ssc[d, n] = top * (1.0 / 32767.0)
            for copy in sends[n, d]:
                copy.start()
        part = product(0, first, second)
        out[:, columns(first)] = part[:, :BLK]
        out[:, columns(second)] = part[:, BLK:]

    def gather(n, first, second):
        for d in range(3):
            for copy in sends[n, d]:
                copy.wait_recv()
            part = rbuf[d, n].astype(jnp.int32).astype(jnp.float32) * rsc[d, n]
            out[:, columns(first)] += part[:, :BLK]
            out[:, columns(second)] += part[:, BLK:]

    near = (gy, xr * 2 + zh)
    nearer = (xl * 2 + zh, xo * 2 + zh)
    distant = (x * 2 + oz, xr * 2 + oz)
    last = (xl * 2 + oz, xo * 2 + oz)

    load_b.wait()
    own_l[0].wait_recv()
    pair(0, *near)
    far_r[0].wait_recv()
    fhop_r[0].start()
    far_l[2].wait_recv()
    fhop_l[2].start()
    far_q[3].wait_recv()
    far_r[3].start()
    far_l[3].start()
    own_r[1].wait_recv()
    hop_r.wait_recv()
    hop_l.wait_recv()
    pair(1, *nearer)
    far_r[1].wait_recv()
    fhop_r[1].start()
    far_l[3].wait_recv()
    fhop_l[3].start()
    far_l[0].wait_recv()
    far_l[1].wait_recv()
    pair(2, *distant)
    far_r[2].wait_recv()
    far_r[3].wait_recv()
    for copy in (fhop_r[0], fhop_r[1], fhop_l[2], fhop_l[3]):
        copy.wait_recv()
    pair(3, *last)
    gather(0, *near)
    gather(1, *nearer)
    gather(2, *distant)
    gather(3, *last)
    for copy in made:
        copy.wait_send()


def shards(attn_out, out_grad, valid_counts):
    any_space = pl.BlockSpec(memory_space=pl.ANY)
    return pl.pallas_call(
        kernel,
        out_shape=jax.ShapeDtypeStruct((2 * BLK, 8 * BLK), jnp.float32),
        in_specs=[pl.BlockSpec(memory_space=pltpu.SMEM), any_space, any_space],
        out_specs=pl.BlockSpec(memory_space=pltpu.VMEM),
        scratch_shapes=[
            pltpu.VMEM((TOK, BLK), jnp.bfloat16),
            pltpu.VMEM((8 * BLK, TOK), jnp.bfloat16),
            pltpu.VMEM((8, TOK, BLK), jnp.bfloat16),
            pltpu.VMEM((3, 4, 2 * BLK, 2 * BLK), jnp.int16),
            pltpu.VMEM((3, 4, 2 * BLK, 2 * BLK), jnp.int16),
            pltpu.VMEM((3, 4, 1, 2 * BLK), jnp.float32),
            pltpu.VMEM((3, 4, 1, 2 * BLK), jnp.float32),
            pltpu.SemaphoreType.DMA((2,)),
            pltpu.SemaphoreType.DMA((COPIES,)),
            pltpu.SemaphoreType.DMA((COPIES,)),
        ],
        compiler_params=pltpu.CompilerParams(
            collective_id=0, has_side_effects=True, vmem_limit_bytes=56 * 1024 * 1024
        ),
        cost_estimate=pl.CostEstimate(
            flops=2 * TOK * 1024 * 1024, bytes_accessed=3 << 20, transcendentals=0
        ),
        name="wgrad",
    )(valid_counts, attn_out, out_grad)


def solution(mesh):
    return jax.shard_map(
        shards,
        mesh=mesh,
        in_specs=(P("gx", ("gy", "gz")), P("gx", ("gz", "gy")), P("gx")),
        out_specs=P(("gy", "gx"), "gz"),
        check_vma=False,
    )
```

time: 345 us -> 105 us (0.30)
  waiting for transfers between devices: 216 us -> 0 us
  Pallas kernels: 0 us -> 101 us
  blocking collectives: 96.5 us -> 0 us
  matrix products: 15.3 us -> 0 us
  between operations: 13.1 us -> 0.01 us
  other arithmetic: 4.42 us -> 0 us
    all_gather x3 -> x0, waiting for transfers between devices: 214 us -> none  [the longest x2 161 us: whole_of(): out = lax.all_gather(out, axes[number], axis=dim, tiled=True)]
    pallas_call x0 -> x1, Pallas kernels: none -> 101 us  [shards(): pl.pallas_call(kernel, out_shape=jax.ShapeDtypeStruct((2 * BLK, 8 * BLK),...]
    all_to_all x1 -> x0, blocking collectives: 96.5 us -> none  [summed_on_arrival(): lax.all_to_all(tiles, axis, split_axis=0, concat_axis=0, tiled=True)]
    dot_general x1 -> x0, matrix products: 15.3 us -> none  [transpose_product(): lax.dot_general(inputs, grads, (((0,), (0,)), ((), ())), preferred_elemen...]
    reduce_sum x1 -> x0, other arithmetic: 3.69 us -> none  [summed_on_arrival(): return arrived.sum(axis=0)]
  transfers between devices with their start and end apart: 3 -> 0, of which waited for: 3 -> 0; matrix products, arithmetic and copies ran while one was open for 0% -> 0% of each run, Pallas kernels for 0% -> 0%
where the time goes in v1:
time: 105 us; the launch traced here: 103 us
  Pallas kernels  101 us (96%)
  local copies, waits for them, and re-layouts  2.31 us (2%)
    pallas_call x1, Pallas kernels, shards(): pl.pallas_call(kernel, out_shape=jax.ShapeDtypeStruct((2 * BLK, 8 * BLK),...  101 us
    unnamed x1, local copies, waits for them, and re-layouts  2.31 us

profile of v1, /device:TPU:8, one launch (start us, length us, event | category | flops | bytes accessed | tf_op | source)
XLA Modules:
  0.0 103.1 jit_solution(18224801208096011806)
XLA Ops:
  0.0 100.8 %wgrad.1 = f32[256,1024]{1,0:T(8,128)} custom-call(s32[4]{0:T(128)} %vc.1, bf16[4096,128]{1,0:T(8,128)(2,1)} %a_hbm.1, bf16[4096,128]{1,0:T(8,128)(2,1)} %b_hbm.1), custom_call_target="tpu_custom_call" | custom-call | flops 8589934592 | bytes 3145728 | tf_op jit(solution)/shard_map/wgrad/pallas_call | solution.py:221
  100.8 2.3 %copy.5 = f32[256,1024]{1,0:T(8,128)} copy(f32[256,1024]{1,0:T(8,128)} %wgrad.1) | data formatting | bytes 2097152

commit v2 on v1

--- a/solution.py
+++ b/solution.py
@@ -13,10 +13,10 @@
 BLK = 128
 CHK = TOK // 4
 HALF = TOK // 2
-COPIES = 64
-
-
-def kernel(vc, a_hbm, b_hbm, out, raw, at, bb, sbuf, rbuf, ssc, rsc, lsem, ss, rs):
+COPIES = 40
+
+
+def kernel(vc, a_hbm, b_hbm, out, raw, at, bb, sbuf, rbuf, ssc, rsc, acc, lsem, ss, rs, pss, prs):
     zl = lax.axis_index("gx")
     gy = lax.axis_index("gy")
     gz = lax.axis_index("gz")
@@ -141,50 +141,114 @@
     for d in range(4):
         sib[d].wait_recv()
 
-    sends = {}
-    for n in range(4):
-        for d in range(3):
-            sends[n, d] = (
-                remote(sbuf.at[d, n], rbuf.at[d, n], owners[d]),
-                remote(ssc.at[d, n], rsc.at[d, n], owners[d]),
+    side = zl // 2
+    mid = (zl + side) % 2
+    end_at, mid_at, far_mid, far_end = 3 * side, 1 + side, 2 - side, 3 - 3 * side
+    goal = [
+        mid * far_mid + (1 - mid) * far_end,
+        mid * end_at + (1 - mid) * far_mid,
+        mid * far_end + (1 - mid) * mid_at,
+    ]
+    goes_to = [
+        mid * far_mid + (1 - mid) * mid_at,
+        mid * end_at + (1 - mid) * far_mid,
+        mid * far_end + (1 - mid) * mid_at,
+    ]
+    lands = [3 * (1 - mid), 1 - mid, 2 - mid]
+
+    blocks = [gy, xr * 2 + zh, xl * 2 + zh, xo * 2 + zh, x * 2 + oz, xr * 2 + oz, xl * 2 + oz, xo * 2 + oz]
+    units = [(0, 2), (2, 2), (4, 2), (6, 1), (7, 1)]
+
+    def part_copies(k, u, slot):
+        first, count = units[u]
+        span = pl.ds(first, count)
+        dev = (goes_to[k], gy, gz)
+        return [
+            pltpu.make_async_remote_copy(
+                src_ref=src.at[k, span],
+                dst_ref=dst.at[slot, span],
+                send_sem=pss.at[k, u, w],
+                recv_sem=prs.at[slot, u, w],
+                device_id=dev,
+                device_id_type=MESH,
             )
+            for w, (src, dst) in enumerate(((sbuf, rbuf), (ssc, rsc)))
+        ]
 
     def columns(slot):
         return pl.ds(pl.multiple_of(slot * BLK, BLK), BLK)
 
-    def product(d, first, second):
-        lhs = at[pl.ds(pl.multiple_of(((zl + d) % 4) * 2 * BLK, 2 * BLK), 2 * BLK), :]
-        rhs = jnp.concatenate([bb[first], bb[second]], axis=1)
-        return jnp.dot(lhs, rhs, preferred_element_type=jnp.float32)
-
-    def pair(n, first, second):
-        for d in range(3):
-            part = product(d + 1, first, second)
-            top = jnp.maximum(jnp.max(jnp.abs(part), axis=0, keepdims=True), 2e-34)
-            sbuf[d, n] = jnp.round(part * (32767.0 / top)).astype(jnp.int32).astype(jnp.int16)
-            ssc[d, n] = top * (1.0 / 32767.0)
-            for copy in sends[n, d]:
-                copy.start()
-        part = product(0, first, second)
-        out[:, columns(first)] = part[:, :BLK]
-        out[:, columns(second)] = part[:, BLK:]
-
-    def gather(n, first, second):
-        for d in range(3):
-            for copy in sends[n, d]:
-                copy.wait_recv()
-            part = rbuf[d, n].astype(jnp.int32).astype(jnp.float32) * rsc[d, n]
-            out[:, columns(first)] += part[:, :BLK]
-            out[:, columns(second)] += part[:, BLK:]
-
-    near = (gy, xr * 2 + zh)
-    nearer = (xl * 2 + zh, xo * 2 + zh)
-    distant = (x * 2 + oz, xr * 2 + oz)
-    last = (xl * 2 + oz, xo * 2 + oz)
+    def product(chunk, u):
+        first, count = units[u]
+        lhs = at[pl.ds(pl.multiple_of(chunk * 2 * BLK, 2 * BLK), 2 * BLK), :]
+        rhs = [bb[blocks[first + i]] for i in range(count)]
+        rhs = rhs[0] if count == 1 else jnp.concatenate(rhs, axis=1)
+        part = jnp.dot(lhs, rhs, preferred_element_type=jnp.float32)
+        return [part[:, i * BLK : (i + 1) * BLK] for i in range(count)]
+
+    def send(k, u, parts):
+        first, count = units[u]
+        for i in range(count):
+            top = jnp.maximum(jnp.max(jnp.abs(parts[i]), axis=0, keepdims=True), 2e-34)
+            sbuf[k, first + i] = jnp.round(parts[i] * (32767.0 / top)).astype(jnp.int32).astype(jnp.int16)
+            ssc[k, first + i] = top * (1.0 / 32767.0)
+        for copy in part_copies(k, u, lands[k]):
+            copy.start()
+
+    def arrived(slot, u):
+        first, count = units[u]
+        for copy in part_copies(0, u, slot):
+            copy.wait_recv()
+        return [
+            rbuf[slot, first + i].astype(jnp.int32).astype(jnp.float32) * rsc[slot, first + i]
+            for i in range(count)
+        ]
+
+    def unit(u):
+        first, count = units[u]
+        for k in (0, 1):
+            send(k, u, product(goal[k], u))
+        parts = product(goal[2], u)
+
+        @pl.when(mid == 0)
+        def _():
+            send(2, u, parts)
+
+        @pl.when(mid == 1)
+        def _():
+            for i in range(count):
+                acc[first + i] = parts[i]
+
+        parts = product(zl, u)
+        for i in range(count):
+            out[:, columns(blocks[first + i])] = parts[i]
+
+    def finish(u):
+        @pl.when(mid == 1)
+        def _():
+            first, count = units[u]
+            parts = arrived(3, u)
+            send(2, u, [acc[first + i] + parts[i] for i in range(count)])
+
+    def gather(u):
+        first, count = units[u]
+
+        def add(slot):
+            parts = arrived(slot, u)
+            for i in range(count):
+                out[:, columns(blocks[first + i])] += parts[i]
+
+        add(0)
+
+        @pl.when(mid == 1)
+        def _():
+            add(2)
+
+        add(1)
 
     load_b.wait()
     own_l[0].wait_recv()
-    pair(0, *near)
+    unit(0)
     far_r[0].wait_recv()
     fhop_r[0].start()
     far_l[2].wait_recv()
@@ -195,25 +259,35 @@
     own_r[1].wait_recv()
     hop_r.wait_recv()
     hop_l.wait_recv()
-    pair(1, *nearer)
+    unit(1)
     far_r[1].wait_recv()
     fhop_r[1].start()
     far_l[3].wait_recv()
     fhop_l[3].start()
+    finish(0)
     far_l[0].wait_recv()
     far_l[1].wait_recv()
-    pair(2, *distant)
+    unit(2)
+    finish(1)
     far_r[2].wait_recv()
     far_r[3].wait_recv()
+    unit(3)
+    finish(2)
+    gather(0)
     for copy in (fhop_r[0], fhop_r[1], fhop_l[2], fhop_l[3]):
         copy.wait_recv()
-    pair(3, *last)
-    gather(0, *near)
-    gather(1, *nearer)
-    gather(2, *distant)
-    gather(3, *last)
+    unit(4)
+    finish(3)
+    gather(1)
+    finish(4)
+    for u in (2, 3, 4):
+        gather(u)
     for copy in made:
         copy.wait_send()
+    for u in range(5):
+        for k in range(3):
+            for copy in part_copies(k, u, 0):
+                copy.wait_send()
 
 
 def shards(attn_out, out_grad, valid_counts):
@@ -227,13 +301,16 @@
             pltpu.VMEM((TOK, BLK), jnp.bfloat16),
             pltpu.VMEM((8 * BLK, TOK), jnp.bfloat16),
             pltpu.VMEM((8, TOK, BLK), jnp.bfloat16),
-            pltpu.VMEM((3, 4, 2 * BLK, 2 * BLK), jnp.int16),
-            pltpu.VMEM((3, 4, 2 * BLK, 2 * BLK), jnp.int16),
-            pltpu.VMEM((3, 4, 1, 2 * BLK), jnp.float32),
-            pltpu.VMEM((3, 4, 1, 2 * BLK), jnp.float32),
+            pltpu.VMEM((3, 8, 2 * BLK, BLK), jnp.int16),
+            pltpu.VMEM((4, 8, 2 * BLK, BLK), jnp.int16),
+            pltpu.VMEM((3, 8, 1, BLK), jnp.float32),
+            pltpu.VMEM((4, 8, 1, BLK), jnp.float32),
+            pltpu.VMEM((8, 2 * BLK, BLK), jnp.float32),
             pltpu.SemaphoreType.DMA((2,)),
             pltpu.SemaphoreType.DMA((COPIES,)),
             pltpu.SemaphoreType.DMA((COPIES,)),
+            pltpu.SemaphoreType.DMA((3, 5, 2)),
+            pltpu.SemaphoreType.DMA((4, 5, 2)),
         ],
         compiler_params=pltpu.CompilerParams(
             collective_id=0, has_side_effects=True, vmem_limit_bytes=56 * 1024 * 1024

time: 105 us -> 101 us (0.962); the launches traced: 103 us -> 101 us
  Pallas kernels: 101 us -> 98.5 us
    pallas_call x1, Pallas kernels: 101 us -> 98.5 us  [shards(): pl.pallas_call(kernel, out_shape=jax.ShapeDtypeStruct((2 * BLK, 8 * BLK),...]
where the time goes in v2:
time: 101 us
  Pallas kernels  98.5 us (98%)
  local copies, waits for them, and re-layouts  2.31 us (2%)
    pallas_call x1, Pallas kernels, shards(): pl.pallas_call(kernel, out_shape=jax.ShapeDtypeStruct((2 * BLK, 8 * BLK),...  98.5 us
    unnamed x1, local copies, waits for them, and re-layouts  2.31 us

profile of v2, /device:TPU:8, one launch (start us, length us, event | category | flops | bytes accessed | tf_op | source)
XLA Modules:
  0.0 100.8 jit_solution(8845813004038822034)
XLA Ops:
  0.0 98.5 %wgrad.1 = f32[256,1024]{1,0:T(8,128)} custom-call(s32[4]{0:T(128)} %vc.1, bf16[4096,128]{1,0:T(8,128)(2,1)} %a_hbm.1, bf16[4096,128]{1,0:T(8,128)(2,1)} %b_hbm.1), custom_call_target="tpu_custom_call" | custom-call | flops 8589934592 | bytes 3145728 | tf_op jit(solution)/shard_map/wgrad/pallas_call | solution.py:295
  98.5 2.3 %copy.5 = f32[256,1024]{1,0:T(8,128)} copy(f32[256,1024]{1,0:T(8,128)} %wgrad.1) | data formatting | bytes 2097152

commit v3 on v2

--- a/solution.py
+++ b/solution.py
@@ -11,12 +11,74 @@
 TOK = 4096
 SEQ = 1024
 BLK = 128
-CHK = TOK // 4
-HALF = TOK // 2
+GRAIN = 32
+CAPS = (2304, 2560, 2816, 3072, 3328, 3584, 4096)
 COPIES = 40
 
 
-def kernel(vc, a_hbm, b_hbm, out, raw, at, bb, sbuf, rbuf, ssc, rsc, acc, lsem, ss, rs, pss, prs):
+def compact(vc, a_hbm, b_hbm, at_out, b_out, which, raw_a, raw_b, mine, theirs, lsem, ss, rs):
+    zl = lax.axis_index("gx")
+    gy = lax.axis_index("gy")
+    gz = lax.axis_index("gz")
+    barrier = pltpu.get_barrier_semaphore()
+    peers = [((zl + d) % 4, gy, gz) for d in range(1, 4)]
+    for dev in peers:
+        pl.semaphore_signal(barrier, inc=1, device_id=dev, device_id_type=MESH)
+    load_a = pltpu.make_async_copy(a_hbm, raw_a, lsem.at[0])
+    load_b = pltpu.make_async_copy(b_hbm, raw_b, lsem.at[1])
+    load_a.start()
+    load_b.start()
+
+    rows_here = TOK // SEQ
+    valid = [vc[r] for r in range(rows_here)]
+    first = [0]
+    for r in range(rows_here):
+        first.append(first[-1] + (valid[r] + GRAIN - 1) // GRAIN)
+    mine[...] = jnp.full(mine.shape, first[-1] * GRAIN, jnp.int32)
+    pl.semaphore_wait(barrier, len(peers))
+    copies = [
+        pltpu.make_async_remote_copy(
+            src_ref=mine, dst_ref=theirs.at[d], send_sem=ss.at[d], recv_sem=rs.at[d],
+            device_id=peers[d], device_id_type=MESH,
+        )
+        for d in range(3)
+    ]
+    for copy in copies:
+        copy.start()
+    load_a.wait()
+    load_b.wait()
+
+    def tile(k, carry):
+        pieces = []
+        for i in range(BLK // GRAIN):
+            n = k * (BLK // GRAIN) + i
+            begin, row, count = first[0], 0, valid[0]
+            for r in range(1, rows_here):
+                past = n >= first[r]
+                begin = jnp.where(past, first[r], begin)
+                row = jnp.where(past, r, row)
+                count = jnp.where(past, valid[r], count)
+            slot = (n - begin) * GRAIN
+            source = jnp.minimum(row * (SEQ // GRAIN) + n - begin, TOK // GRAIN - 1)
+            kept = lax.broadcasted_iota(jnp.int32, (GRAIN, BLK), 0) + slot < count
+            piece = raw_a[source]
+            pieces.append(jnp.where(kept, piece, jnp.zeros((), piece.dtype)))
+            b_out[pl.ds(pl.multiple_of(n * GRAIN, GRAIN), GRAIN), :] = raw_b[source]
+        span = pl.ds(pl.multiple_of(k * BLK, BLK), BLK)
+        at_out[:, span] = jnp.concatenate(pieces, axis=0).T
+        return carry
+
+    lax.fori_loop(0, TOK // BLK, tile, 0)
+    for copy in copies:
+        copy.wait_recv()
+    most = jnp.maximum(jnp.maximum(mine[...], theirs[0]), jnp.maximum(theirs[1], theirs[2]))
+    which[...] = sum(jnp.where(most > cap, 1, 0) for cap in CAPS[:-1])
+    for copy in copies:
+        copy.wait_send()
+
+
+def kernel(cap, a_hbm, b_hbm, out, at, bb, sbuf, rbuf, ssc, rsc, acc, lsem, ss, rs, pss, prs):
+    CHK, HALF = cap // 4, cap // 2
     zl = lax.axis_index("gx")
     gy = lax.axis_index("gy")
     gz = lax.axis_index("gz")
@@ -28,7 +90,6 @@
     right, left = (zl, xr * 2 + zh, gz), (zl, xl * 2 + zh, gz)
     far = (zl, x * 2 + (1 - zh), gz)
     up, down = (zl, gy, yr * 2 + c), (zl, gy, yl * 2 + c)
-    opposite = (zl, gy, yo * 2 + c)
     sibling = (zl, gy, y * 2 + (1 - c))
     owners = [((zl + d) % 4, gy, gz) for d in range(1, 4)]
 
@@ -37,8 +98,13 @@
     for dev in partners:
         pl.semaphore_signal(barrier, inc=1, device_id=dev, device_id_type=MESH)
 
-    load_a = pltpu.make_async_copy(a_hbm, raw, lsem.at[0])
-    load_b = pltpu.make_async_copy(b_hbm, bb.at[gy], lsem.at[1])
+    def rows(block, h=None):
+        if h is None:
+            return pl.ds(pl.multiple_of(block * BLK, BLK), BLK)
+        return pl.ds(pl.multiple_of(block * BLK + h * (BLK // 2), BLK // 2), BLK // 2)
+
+    load_a = pltpu.make_async_copy(a_hbm.at[:, pl.ds(0, cap)], at.at[rows(gz)], lsem.at[0])
+    load_b = pltpu.make_async_copy(b_hbm.at[pl.ds(0, cap)], bb.at[gy], lsem.at[1])
     load_a.start()
     load_b.start()
     pl.semaphore_wait(barrier, len(partners))
@@ -76,19 +142,19 @@
     fhop_r = {q: relay(xl * 2 + oz, q, CHK, right) for q in (0, 1)}
     fhop_l = {q: relay(xr * 2 + oz, q, CHK, left) for q in (2, 3)}
 
-    def rows(block, h=None):
-        if h is None:
-            return pl.ds(pl.multiple_of(block * BLK, BLK), BLK)
-        return pl.ds(pl.multiple_of(block * BLK + h * (BLK // 2), BLK // 2), BLK // 2)
-
     def pass_on(block, h, dev):
         return remote(at.at[rows(block, h)], at.at[rows(block, h)], dev)
 
-    a_up = {h: pass_on(gz, h, up) for h in range(2)}
-    a_down = {h: pass_on(gz, h, down) for h in range(2)}
+    def own(h, dev):
+        part = pl.ds(h * (BLK // 2), BLK // 2)
+        return remote(a_hbm.at[part, pl.ds(0, cap)], at.at[rows(gz, h)], dev)
+
+    a_up = {h: own(h, up) for h in range(2)}
+    a_down = {h: own(h, down) for h in range(2)}
     ahop_up = pass_on(yl * 2 + c, 0, up)
     ahop_down = pass_on(yr * 2 + c, 1, down)
-    sib = {d: pass_on(((y + d) % 4) * 2 + c, None, sibling) for d in range(4)}
+    sib = {d: pass_on(((y + d) % 4) * 2 + c, None, sibling) for d in range(1, 4)}
+    sib[0] = remote(a_hbm.at[:, pl.ds(0, cap)], at.at[rows(gz)], sibling)
 
     for q in (0, 2, 1, 3):
         far_q[q].start()
@@ -97,17 +163,6 @@
     own_r[1].start()
     own_l[0].start()
 
-    load_a.wait()
-
-    def turn(k, carry):
-        lanes = lax.broadcasted_iota(jnp.int32, (BLK, BLK), 1) + (k % (SEQ // BLK)) * BLK
-        kept = lanes < vc[k // (SEQ // BLK)]
-        span = pl.ds(pl.multiple_of(k * BLK, BLK), BLK)
-        tile = raw[span, :].T
-        at[rows(gz), span] = jnp.where(kept, tile, jnp.zeros((), tile.dtype))
-        return carry
-
-    lax.fori_loop(0, TOK // BLK, turn, 0)
     a_up[0].start()
     a_down[1].start()
     a_up[1].start()
@@ -118,26 +173,26 @@
     hop_r.start()
     own_l[1].wait_recv()
     hop_l.start()
-    far_q[0].wait_recv()
-    far_r[0].start()
-    far_l[0].start()
     a_up[0].wait_recv()
     ahop_up.start()
     a_down[1].wait_recv()
     ahop_down.start()
-    far_q[2].wait_recv()
-    far_r[2].start()
-    far_l[2].start()
+    far_q[0].wait_recv()
+    far_r[0].start()
+    far_l[0].start()
     a_up[1].wait_recv()
     sib[3].start()
     a_down[0].wait_recv()
     sib[1].start()
+    far_q[2].wait_recv()
+    far_r[2].start()
+    far_l[2].start()
+    ahop_up.wait_recv()
+    ahop_down.wait_recv()
+    sib[2].start()
     far_q[1].wait_recv()
     far_r[1].start()
     far_l[1].start()
-    ahop_up.wait_recv()
-    ahop_down.wait_recv()
-    sib[2].start()
     for d in range(4):
         sib[d].wait_recv()
 
@@ -159,10 +214,18 @@
     blocks = [gy, xr * 2 + zh, xl * 2 + zh, xo * 2 + zh, x * 2 + oz, xr * 2 + oz, xl * 2 + oz, xo * 2 + oz]
     units = [(0, 2), (2, 2), (4, 2), (6, 1), (7, 1)]
 
+    def pick(choices, k):
+        if isinstance(k, int):
+            return choices[k]
+        value = choices[-1]
+        for i in range(len(choices) - 1):
+            value = jnp.where(k == i, choices[i], value)
+        return value
+
     def part_copies(k, u, slot):
         first, count = units[u]
         span = pl.ds(first, count)
-        dev = (goes_to[k], gy, gz)
+        dev = (pick(goes_to, k), gy, gz)
         return [
             pltpu.make_async_remote_copy(
                 src_ref=src.at[k, span],
@@ -192,7 +255,7 @@
             top = jnp.maximum(jnp.max(jnp.abs(parts[i]), axis=0, keepdims=True), 2e-34)
             sbuf[k, first + i] = jnp.round(parts[i] * (32767.0 / top)).astype(jnp.int32).astype(jnp.int16)
             ssc[k, first + i] = top * (1.0 / 32767.0)
-        for copy in part_copies(k, u, lands[k]):
+        for copy in part_copies(k, u, pick(lands, k)):
             copy.start()
 
     def arrived(slot, u):
@@ -206,22 +269,28 @@
 
     def unit(u):
         first, count = units[u]
-        for k in (0, 1):
-            send(k, u, product(goal[k], u))
-        parts = product(goal[2], u)
-
-        @pl.when(mid == 0)
-        def _():
-            send(2, u, parts)
-
-        @pl.when(mid == 1)
-        def _():
-            for i in range(count):
-                acc[first + i] = parts[i]
-
-        parts = product(zl, u)
-        for i in range(count):
-            out[:, columns(blocks[first + i])] = parts[i]
+
+        def step(k, carry):
+            parts = product(pick(goal + [zl], k), u)
+            held = jnp.logical_and(k == 2, mid == 1)
+
+            @pl.when(jnp.logical_and(k < 3, jnp.logical_not(held)))
+            def _():
+                send(k, u, parts)
+
+            @pl.when(held)
+            def _():
+                for i in range(count):
+                    acc[first + i] = parts[i]
+
+            @pl.when(k == 3)
+            def _():
+                for i in range(count):
+                    out[:, columns(blocks[first + i])] = parts[i]
+
+            return carry
+
+        lax.fori_loop(0, 4, step, 0)
 
     def finish(u):
         @pl.when(mid == 1)
@@ -246,16 +315,17 @@
 
         add(1)
 
+    load_a.wait()
     load_b.wait()
     own_l[0].wait_recv()
     unit(0)
+    far_q[3].wait_recv()
+    far_r[3].start()
+    far_l[3].start()
     far_r[0].wait_recv()
     fhop_r[0].start()
     far_l[2].wait_recv()
     fhop_l[2].start()
-    far_q[3].wait_recv()
-    far_r[3].start()
-    far_l[3].start()
     own_r[1].wait_recv()
     hop_r.wait_recv()
     hop_l.wait_recv()
@@ -264,9 +334,9 @@
     fhop_r[1].start()
     far_l[3].wait_recv()
     fhop_l[3].start()
-    finish(0)
     far_l[0].wait_recv()
     far_l[1].wait_recv()
+    finish(0)
     unit(2)
     finish(1)
     far_r[2].wait_recv()
@@ -274,14 +344,17 @@
     unit(3)
     finish(2)
     gather(0)
-    for copy in (fhop_r[0], fhop_r[1], fhop_l[2], fhop_l[3]):
-        copy.wait_recv()
+    fhop_r[0].wait_recv()
+    fhop_r[1].wait_recv()
+    fhop_l[2].wait_recv()
+    fhop_l[3].wait_recv()
     unit(4)
     finish(3)
     gather(1)
     finish(4)
-    for u in (2, 3, 4):
-        gather(u)
+    gather(2)
+    gather(3)
+    gather(4)
     for copy in made:
         copy.wait_send()
     for u in range(5):
@@ -290,17 +363,16 @@
                 copy.wait_send()
 
 
-def shards(attn_out, out_grad, valid_counts):
+def main(cap, number):
     any_space = pl.BlockSpec(memory_space=pl.ANY)
     return pl.pallas_call(
-        kernel,
+        functools.partial(kernel, cap),
         out_shape=jax.ShapeDtypeStruct((2 * BLK, 8 * BLK), jnp.float32),
-        in_specs=[pl.BlockSpec(memory_space=pltpu.SMEM), any_space, any_space],
+        in_specs=[any_space, any_space],
         out_specs=pl.BlockSpec(memory_space=pltpu.VMEM),
         scratch_shapes=[
-            pltpu.VMEM((TOK, BLK), jnp.bfloat16),
-            pltpu.VMEM((8 * BLK, TOK), jnp.bfloat16),
-            pltpu.VMEM((8, TOK, BLK), jnp.bfloat16),
+            pltpu.VMEM((8 * BLK, cap), jnp.bfloat16),
+            pltpu.VMEM((8, cap, BLK), jnp.bfloat16),
             pltpu.VMEM((3, 8, 2 * BLK, BLK), jnp.int16),
             pltpu.VMEM((4, 8, 2 * BLK, BLK), jnp.int16),
             pltpu.VMEM((3, 8, 1, BLK), jnp.float32),
@@ -313,13 +385,44 @@
             pltpu.SemaphoreType.DMA((4, 5, 2)),
         ],
         compiler_params=pltpu.CompilerParams(
-            collective_id=0, has_side_effects=True, vmem_limit_bytes=56 * 1024 * 1024
+            collective_id=number, has_side_effects=True, vmem_limit_bytes=48 * 1024 * 1024
         ),
         cost_estimate=pl.CostEstimate(
-            flops=2 * TOK * 1024 * 1024, bytes_accessed=3 << 20, transcendentals=0
+            flops=2 * cap * 1024 * 1024, bytes_accessed=3 << 20, transcendentals=0
         ),
-        name="wgrad",
-    )(valid_counts, attn_out, out_grad)
+        name=f"wgrad{cap}",
+    )
+
+
+def shards(attn_out, out_grad, valid_counts):
+    hbm = pl.BlockSpec(memory_space=pltpu.HBM)
+    vmem = pl.BlockSpec(memory_space=pltpu.VMEM)
+    grains = [value.reshape(TOK // GRAIN, GRAIN, BLK) for value in (attn_out, out_grad)]
+    turned, packed, which = pl.pallas_call(
+        compact,
+        out_shape=(
+            jax.ShapeDtypeStruct((BLK, TOK), attn_out.dtype),
+            jax.ShapeDtypeStruct((TOK, BLK), out_grad.dtype),
+            jax.ShapeDtypeStruct((8, BLK), jnp.int32),
+        ),
+        in_specs=[pl.BlockSpec(memory_space=pltpu.SMEM), hbm, hbm],
+        out_specs=(vmem, vmem, vmem),
+        scratch_shapes=[
+            pltpu.VMEM((TOK // GRAIN, GRAIN, BLK), jnp.bfloat16),
+            pltpu.VMEM((TOK // GRAIN, GRAIN, BLK), jnp.bfloat16),
+            pltpu.VMEM((8, BLK), jnp.int32),
+            pltpu.VMEM((3, 8, BLK), jnp.int32),
+            pltpu.SemaphoreType.DMA((3,)),
+            pltpu.SemaphoreType.DMA((3,)),
+            pltpu.SemaphoreType.DMA((3,)),
+        ],
+        compiler_params=pltpu.CompilerParams(
+            collective_id=0, has_side_effects=True, vmem_limit_bytes=16 * 1024 * 1024
+        ),
+        name="compact",
+    )(valid_counts, *(pltpu.with_memory_space_constraint(value, pltpu.HBM) for value in grains))
+    branches = [main(cap, 1 + i) for i, cap in enumerate(CAPS)]
+    return lax.switch(which[0, 0], branches, turned, packed)
 
 
 def solution(mesh):

time: 101 us -> 86.2 us (0.85)
  Pallas kernels: 98.5 us -> 82.5 us
    pallas_call x1 -> x2, Pallas kernels: 98.5 us -> 82.5 us  [the longest x1 74.3 us: shards(): return lax.switch(which[0, 0], branches, turned, packed)]
    unnamed x1 -> x3, local copies, waits for them, and re-layouts: 2.31 us -> 1.63 us
where the time goes in v3:
time: 86.2 us; the launch traced here: 85.8 us
  Pallas kernels  82.5 us (96%)
  local copies, waits for them, and re-layouts  2.14 us (2%)
    pallas_call x1, Pallas kernels, shards(): return lax.switch(which[0, 0], branches, turned, packed)  74.3 us
    pallas_call x1, Pallas kernels, shards(): pl.pallas_call(compact, out_shape=(jax.ShapeDtypeStruct((BLK, TOK), attn_...  8.24 us

profile of v3, /device:TPU:8, one launch (start us, length us, event | category | flops | bytes accessed | tf_op | source)
XLA Modules:
  0.0 85.8 jit_solution(12247453913990488000)
XLA Ops:
  0.0 0.0 copy-start
  0.0 0.7 copy-done
  0.7 8.2 %compact.1 = (bf16[128,4096]{1,0:T(8,128)(2,1)S(1)}, bf16[4096,128]{1,0:T(8,128)(2,1)S(1)}, s32[8,128]{1,0:T(8,128)S(1)}) custom-call(s32[4]{0:T(128)S(1)} %copy-done, bf16[128,32,128]{2,1,0:T(8,128)(2,1)} %bitcast.3, bf16[128,32,128]{2,1,0:T(8,128)(2,1)} %bitcast.4), custom_call_target="tpu_custom_call" | custom-call | tf_op jit(solution)/shard_map/compact/pallas_call | solution.py:401
  8.9 0.5 slice.3
  10.1 74.8 %conditional.1 = (f32[256,1024]{1,0:T(8,128)S(1)}) conditional(s32[]{:T(128)} %bitcast.2, (bf16[128,4096]{1,0:T(8,128)(2,1)S(1)}, bf16[4096,128]{1,0:T(8,128)(2,1)S(1)}) %tuple.26, (bf16[128,4096]{1,0:T(8,128)(2,1)S(1)}, bf16[4096,128]{1,0:T(8,128)(2,1)S(1)}) %tuple.26, (bf16[128,4096]{1,0:T(8,128)(2,1)S(1)}, ...), branch_computations={%region_0.0_spmd, %region_1.0_spmd, %region_2.0_spmd, %region_3.0_... | conditional | flops 8589934592 | bytes 3145736 | solution.py:425
  10.1 74.3 %wgrad2816.1 = f32[256,1024]{1,0:T(8,128)S(1)} custom-call(bf16[128,4096]{1,0:T(8,128)(2,1)S(1)} %get-tuple-element.44.a_hbm, bf16[4096,128]{1,0:T(8,128)(2,1)S(1)} %get-tuple-element.46.b_hbm), custom_call_target="tpu_custom_call" | custom-call | flops 5905580032 | bytes 3145728 | tf_op jit(solution)/shard_map/cond/branch_2_fun/wgrad2816/pallas_call | solution.py:425
  84.8 1.0 %copy.19 = f32[256,1024]{1,0:T(8,128)} copy(f32[256,1024]{1,0:T(8,128)S(1)} %get-tuple-element.61) | data formatting | bytes 2097152
Async XLA Ops:
  0.0 0.7 copy-start

commit v4 on v3

--- a/solution.py
+++ b/solution.py
@@ -12,24 +12,30 @@
 SEQ = 1024
 BLK = 128
 GRAIN = 32
-CAPS = (2304, 2560, 2816, 3072, 3328, 3584, 4096)
-COPIES = 40
-
-
-def compact(vc, a_hbm, b_hbm, at_out, b_out, which, raw_a, raw_b, mine, theirs, lsem, ss, rs):
+CAPS = (2432, 2560, 2688, 2816, 2944, 3072, 3200, 3328, 3584, 4096)
+UNROLL = 4
+COPIES = 32
+
+
+def compact(vc_hbm, a_hbm, b_hbm, at_out, b_out, which, vc, raw_a, raw_b, mine, theirs, csem, lsem, ss, rs):
     zl = lax.axis_index("gx")
     gy = lax.axis_index("gy")
     gz = lax.axis_index("gz")
+    rows_here = TOK // SEQ
     barrier = pltpu.get_barrier_semaphore()
     peers = [((zl + d) % 4, gy, gz) for d in range(1, 4)]
     for dev in peers:
         pl.semaphore_signal(barrier, inc=1, device_id=dev, device_id_type=MESH)
-    load_a = pltpu.make_async_copy(a_hbm, raw_a, lsem.at[0])
-    load_b = pltpu.make_async_copy(b_hbm, raw_b, lsem.at[1])
-    load_a.start()
-    load_b.start()
-
-    rows_here = TOK // SEQ
+    counts = pltpu.make_async_copy(vc_hbm, vc, csem)
+    counts.start()
+    loads = []
+    for r in range(rows_here):
+        part = pl.ds(r * (SEQ // GRAIN), SEQ // GRAIN)
+        loads.append(pltpu.make_async_copy(a_hbm.at[part], raw_a.at[part], lsem.at[0, r]))
+        loads.append(pltpu.make_async_copy(b_hbm.at[part], raw_b.at[part], lsem.at[1, r]))
+    for load in loads:
+        load.start()
+    counts.wait()
     valid = [vc[r] for r in range(rows_here)]
     first = [0]
     for r in range(rows_here):
@@ -45,10 +51,10 @@
     ]
     for copy in copies:
         copy.start()
-    load_a.wait()
-    load_b.wait()
-
-    def tile(k, carry):
+    for load in loads:
+        load.wait()
+
+    def tile(k):
         pieces = []
         for i in range(BLK // GRAIN):
             n = k * (BLK // GRAIN) + i
@@ -58,26 +64,35 @@
                 begin = jnp.where(past, first[r], begin)
                 row = jnp.where(past, r, row)
                 count = jnp.where(past, valid[r], count)
-            slot = (n - begin) * GRAIN
-            source = jnp.minimum(row * (SEQ // GRAIN) + n - begin, TOK // GRAIN - 1)
-            kept = lax.broadcasted_iota(jnp.int32, (GRAIN, BLK), 0) + slot < count
+            slot = n - begin
+            source = jnp.minimum(row * (SEQ // GRAIN) + slot, TOK // GRAIN - 1)
+            kept = lax.broadcasted_iota(jnp.int32, (GRAIN, BLK), 0) + slot * GRAIN < count
             piece = raw_a[source]
             pieces.append(jnp.where(kept, piece, jnp.zeros((), piece.dtype)))
             b_out[pl.ds(pl.multiple_of(n * GRAIN, GRAIN), GRAIN), :] = raw_b[source]
         span = pl.ds(pl.multiple_of(k * BLK, BLK), BLK)
         at_out[:, span] = jnp.concatenate(pieces, axis=0).T
+
+    def tiles(k, carry):
+        for i in range(UNROLL):
+            tile(k * UNROLL + i)
         return carry
 
-    lax.fori_loop(0, TOK // BLK, tile, 0)
+    lax.fori_loop(0, TOK // BLK // UNROLL, tiles, 0)
     for copy in copies:
         copy.wait_recv()
-    most = jnp.maximum(jnp.maximum(mine[...], theirs[0]), jnp.maximum(theirs[1], theirs[2]))
-    which[...] = sum(jnp.where(most > cap, 1, 0) for cap in CAPS[:-1])
+    most = first[-1] * GRAIN
+    for d in range(3):
+        most = jnp.maximum(most, theirs[d, 0, 0])
+    index = 0
+    for cap in CAPS[:-1]:
+        index = index + jnp.where(most > cap, 1, 0)
+    which[0] = index
     for copy in copies:
         copy.wait_send()
 
 
-def kernel(cap, a_hbm, b_hbm, out, at, bb, sbuf, rbuf, ssc, rsc, acc, lsem, ss, rs, pss, prs):
+def kernel(cap, a_hbm, b_hbm, result, out, at, bb, sbuf, rbuf, ssc, rsc, acc, lsem, osem, sent, rs, prs):
     CHK, HALF = cap // 4, cap // 2
     zl = lax.axis_index("gx")
     gy = lax.axis_index("gy")
@@ -111,12 +126,12 @@
 
     made = []
 
-    def remote(src, dst, dev):
+    def remote(src, dst, dev, kind=0):
         k = len(made)
         copy = pltpu.make_async_remote_copy(
             src_ref=src,
             dst_ref=dst,
-            send_sem=ss.at[k],
+            send_sem=sent.at[kind],
             recv_sem=rs.at[k],
             device_id=dev,
             device_id_type=MESH,
@@ -143,18 +158,18 @@
     fhop_l = {q: relay(xr * 2 + oz, q, CHK, left) for q in (2, 3)}
 
     def pass_on(block, h, dev):
-        return remote(at.at[rows(block, h)], at.at[rows(block, h)], dev)
+        return remote(at.at[rows(block, h)], at.at[rows(block, h)], dev, 1)
 
     def own(h, dev):
         part = pl.ds(h * (BLK // 2), BLK // 2)
-        return remote(a_hbm.at[part, pl.ds(0, cap)], at.at[rows(gz, h)], dev)
+        return remote(a_hbm.at[part, pl.ds(0, cap)], at.at[rows(gz, h)], dev, 1)
 
     a_up = {h: own(h, up) for h in range(2)}
     a_down = {h: own(h, down) for h in range(2)}
     ahop_up = pass_on(yl * 2 + c, 0, up)
     ahop_down = pass_on(yr * 2 + c, 1, down)
     sib = {d: pass_on(((y + d) % 4) * 2 + c, None, sibling) for d in range(1, 4)}
-    sib[0] = remote(a_hbm.at[:, pl.ds(0, cap)], at.at[rows(gz)], sibling)
+    sib[0] = remote(a_hbm.at[:, pl.ds(0, cap)], at.at[rows(gz)], sibling, 1)
 
     for q in (0, 2, 1, 3):
         far_q[q].start()
@@ -212,7 +227,6 @@
     lands = [3 * (1 - mid), 1 - mid, 2 - mid]
 
     blocks = [gy, xr * 2 + zh, xl * 2 + zh, xo * 2 + zh, x * 2 + oz, xr * 2 + oz, xl * 2 + oz, xo * 2 + oz]
-    units = [(0, 2), (2, 2), (4, 2), (6, 1), (7, 1)]
 
     def pick(choices, k):
         if isinstance(k, int):
@@ -223,14 +237,13 @@
         return value
 
     def part_copies(k, u, slot):
-        first, count = units[u]
-        span = pl.ds(first, count)
+        span = pl.ds(2 * u, 2)
         dev = (pick(goes_to, k), gy, gz)
         return [
             pltpu.make_async_remote_copy(
                 src_ref=src.at[k, span],
                 dst_ref=dst.at[slot, span],
-                send_sem=pss.at[k, u, w],
+                send_sem=sent.at[2 + w],
                 recv_sem=prs.at[slot, u, w],
                 device_id=dev,
                 device_id_type=MESH,
@@ -238,38 +251,32 @@
             for w, (src, dst) in enumerate(((sbuf, rbuf), (ssc, rsc)))
         ]
 
-    def columns(slot):
-        return pl.ds(pl.multiple_of(slot * BLK, BLK), BLK)
+    def columns(u, i):
+        return pl.ds(pl.multiple_of(pick(blocks[i::2], u) * BLK, BLK), BLK)
 
     def product(chunk, u):
-        first, count = units[u]
         lhs = at[pl.ds(pl.multiple_of(chunk * 2 * BLK, 2 * BLK), 2 * BLK), :]
-        rhs = [bb[blocks[first + i]] for i in range(count)]
-        rhs = rhs[0] if count == 1 else jnp.concatenate(rhs, axis=1)
+        rhs = jnp.concatenate([bb[pick(blocks[i::2], u)] for i in range(2)], axis=1)
         part = jnp.dot(lhs, rhs, preferred_element_type=jnp.float32)
-        return [part[:, i * BLK : (i + 1) * BLK] for i in range(count)]
+        return [part[:, :BLK], part[:, BLK:]]
 
     def send(k, u, parts):
-        first, count = units[u]
-        for i in range(count):
+        for i in range(2):
             top = jnp.maximum(jnp.max(jnp.abs(parts[i]), axis=0, keepdims=True), 2e-34)
-            sbuf[k, first + i] = jnp.round(parts[i] * (32767.0 / top)).astype(jnp.int32).astype(jnp.int16)
-            ssc[k, first + i] = top * (1.0 / 32767.0)
+            sbuf[k, 2 * u + i] = jnp.round(parts[i] * (32767.0 / top)).astype(jnp.int32).astype(jnp.int16)
+            ssc[k, 2 * u + i] = top * (1.0 / 32767.0)
         for copy in part_copies(k, u, pick(lands, k)):
             copy.start()
 
     def arrived(slot, u):
-        first, count = units[u]
         for copy in part_copies(0, u, slot):
             copy.wait_recv()
         return [
-            rbuf[slot, first + i].astype(jnp.int32).astype(jnp.float32) * rsc[slot, first + i]
-            for i in range(count)
+            rbuf[slot, 2 * u + i].astype(jnp.int32).astype(jnp.float32) * rsc[slot, 2 * u + i]
+            for i in range(2)
         ]
 
     def unit(u):
-        first, count = units[u]
-
         def step(k, carry):
             parts = product(pick(goal + [zl], k), u)
             held = jnp.logical_and(k == 2, mid == 1)
@@ -280,32 +287,33 @@
 
             @pl.when(held)
             def _():
-                for i in range(count):
-                    acc[first + i] = parts[i]
+                for i in range(2):
+                    acc[2 * u + i] = parts[i]
 
             @pl.when(k == 3)
             def _():
-                for i in range(count):
-                    out[:, columns(blocks[first + i])] = parts[i]
+                for i in range(2):
+                    out[:, columns(u, i)] = parts[i]
 
             return carry
 
         lax.fori_loop(0, 4, step, 0)
 
     def finish(u):
-        @pl.when(mid == 1)
-        def _():
-            first, count = units[u]
-            parts = arrived(3, u)
-            send(2, u, [acc[first + i] + parts[i] for i in range(count)])
-
-    def gather(u):
-        first, count = units[u]
-
+        parts = arrived(3, u)
+        send(2, u, [acc[2 * u + i] + parts[i] for i in range(2)])
+
+    def stores(u):
+        return [
+            pltpu.make_async_copy(out.at[:, columns(u, i)], result.at[:, columns(u, i)], osem)
+            for i in range(2)
+        ]
+
+    def gather(u, carry):
         def add(slot):
             parts = arrived(slot, u)
-            for i in range(count):
-                out[:, columns(blocks[first + i])] += parts[i]
+            for i in range(2):
+                out[:, columns(u, i)] += parts[i]
 
         add(0)
 
@@ -314,53 +322,68 @@
             add(2)
 
         add(1)
-
-    load_a.wait()
-    load_b.wait()
-    own_l[0].wait_recv()
-    unit(0)
-    far_q[3].wait_recv()
-    far_r[3].start()
-    far_l[3].start()
-    far_r[0].wait_recv()
-    fhop_r[0].start()
-    far_l[2].wait_recv()
-    fhop_l[2].start()
-    own_r[1].wait_recv()
-    hop_r.wait_recv()
-    hop_l.wait_recv()
-    unit(1)
-    far_r[1].wait_recv()
-    fhop_r[1].start()
-    far_l[3].wait_recv()
-    fhop_l[3].start()
-    far_l[0].wait_recv()
-    far_l[1].wait_recv()
-    finish(0)
-    unit(2)
-    finish(1)
-    far_r[2].wait_recv()
-    far_r[3].wait_recv()
-    unit(3)
-    finish(2)
-    gather(0)
-    fhop_r[0].wait_recv()
-    fhop_r[1].wait_recv()
-    fhop_l[2].wait_recv()
-    fhop_l[3].wait_recv()
-    unit(4)
-    finish(3)
-    gather(1)
-    finish(4)
-    gather(2)
-    gather(3)
-    gather(4)
-    for copy in made:
-        copy.wait_send()
-    for u in range(5):
-        for k in range(3):
-            for copy in part_copies(k, u, 0):
-                copy.wait_send()
+        for copy in stores(u):
+            copy.start()
+        return carry
+
+    def stage(u, carry):
+        @pl.when(u == 0)
+        def _():
+            load_a.wait()
+            load_b.wait()
+            own_l[0].wait_recv()
+
+        @pl.when(u == 1)
+        def _():
+            far_q[3].wait_recv()
+            far_r[3].start()
+            far_l[3].start()
+            far_r[0].wait_recv()
+            fhop_r[0].start()
+            far_l[2].wait_recv()
+            fhop_l[2].start()
+            own_r[1].wait_recv()
+            hop_r.wait_recv()
+            hop_l.wait_recv()
+
+        @pl.when(u == 2)
+        def _():
+            far_r[1].wait_recv()
+            fhop_r[1].start()
+            far_l[3].wait_recv()
+            fhop_l[3].start()
+            far_l[0].wait_recv()
+            far_l[1].wait_recv()
+
+        @pl.when(u == 3)
+        def _():
+            far_r[2].wait_recv()
+            far_r[3].wait_recv()
+            fhop_r[0].wait_recv()
+            fhop_r[1].wait_recv()
+            fhop_l[2].wait_recv()
+            fhop_l[3].wait_recv()
+
+        unit(u)
+
+        @pl.when(jnp.logical_and(u > 0, mid == 1))
+        def _():
+            finish(u - 1)
+
+        return carry
+
+    lax.fori_loop(0, 4, stage, 0)
+
+    @pl.when(mid == 1)
+    def _():
+        finish(3)
+
+    lax.fori_loop(0, 4, gather, 0)
+    pltpu.make_async_copy(out, result, osem).wait()
+    pltpu.make_async_copy(bb.at[pl.ds(0, 7)], bb.at[pl.ds(0, 7)], sent.at[0]).wait()
+    pltpu.make_async_copy(at.at[pl.ds(0, 7 * BLK)], at.at[pl.ds(0, 7 * BLK)], sent.at[1]).wait()
+    pltpu.make_async_copy(sbuf, sbuf, sent.at[2]).wait()
+    pltpu.make_async_copy(ssc, ssc, sent.at[3]).wait()
 
 
 def main(cap, number):
@@ -368,9 +391,10 @@
     return pl.pallas_call(
         functools.partial(kernel, cap),
         out_shape=jax.ShapeDtypeStruct((2 * BLK, 8 * BLK), jnp.float32),
-        in_specs=[any_space, any_space],
-        out_specs=pl.BlockSpec(memory_space=pltpu.VMEM),
+        in_specs=[any_space] * 2,
+        out_specs=any_space,
         scratch_shapes=[
+            pltpu.VMEM((2 * BLK, 8 * BLK), jnp.float32),
             pltpu.VMEM((8 * BLK, cap), jnp.bfloat16),
             pltpu.VMEM((8, cap, BLK), jnp.bfloat16),
             pltpu.VMEM((3, 8, 2 * BLK, BLK), jnp.int16),
@@ -379,10 +403,10 @@
             pltpu.VMEM((4, 8, 1, BLK), jnp.float32),
             pltpu.VMEM((8, 2 * BLK, BLK), jnp.float32),
             pltpu.SemaphoreType.DMA((2,)),
+            pltpu.SemaphoreType.DMA,
+            pltpu.SemaphoreType.DMA((4,)),
             pltpu.SemaphoreType.DMA((COPIES,)),
-            pltpu.SemaphoreType.DMA((COPIES,)),
-            pltpu.SemaphoreType.DMA((3, 5, 2)),
-            pltpu.SemaphoreType.DMA((4, 5, 2)),
+            pltpu.SemaphoreType.DMA((4, 4, 2)),
         ],
         compiler_params=pltpu.CompilerParams(
             collective_id=number, has_side_effects=True, vmem_limit_bytes=48 * 1024 * 1024
@@ -403,16 +427,18 @@
         out_shape=(
             jax.ShapeDtypeStruct((BLK, TOK), attn_out.dtype),
             jax.ShapeDtypeStruct((TOK, BLK), out_grad.dtype),
-            jax.ShapeDtypeStruct((8, BLK), jnp.int32),
+            jax.ShapeDtypeStruct((1,), jnp.int32),
         ),
-        in_specs=[pl.BlockSpec(memory_space=pltpu.SMEM), hbm, hbm],
-        out_specs=(vmem, vmem, vmem),
+        in_specs=[hbm, hbm, hbm],
+        out_specs=(vmem, vmem, pl.BlockSpec(memory_space=pltpu.SMEM)),
         scratch_shapes=[
+            pltpu.SMEM((TOK // SEQ,), jnp.int32),
             pltpu.VMEM((TOK // GRAIN, GRAIN, BLK), jnp.bfloat16),
             pltpu.VMEM((TOK // GRAIN, GRAIN, BLK), jnp.bfloat16),
             pltpu.VMEM((8, BLK), jnp.int32),
             pltpu.VMEM((3, 8, BLK), jnp.int32),
-            pltpu.SemaphoreType.DMA((3,)),
+            pltpu.SemaphoreType.DMA,
+            pltpu.SemaphoreType.DMA((2, TOK // SEQ)),
             pltpu.SemaphoreType.DMA((3,)),
             pltpu.SemaphoreType.DMA((3,)),
         ],
@@ -420,9 +446,9 @@
             collective_id=0, has_side_effects=True, vmem_limit_bytes=16 * 1024 * 1024
         ),
         name="compact",
-    )(valid_counts, *(pltpu.with_memory_space_constraint(value, pltpu.HBM) for value in grains))
+    )(*(pltpu.with_memory_space_constraint(value, pltpu.HBM) for value in (valid_counts, *grains)))
     branches = [main(cap, 1 + i) for i, cap in enumerate(CAPS)]
-    return lax.switch(which[0, 0], branches, turned, packed)
+    return lax.switch(which[0], branches, turned, packed)
 
 
 def solution(mesh):

time: 86.2 us -> 85 us (0.986)
  local copies, waits for them, and re-layouts: 2.14 us -> 0.97 us
where the time goes in v4:
time: 85 us; the launch traced here: 84.2 us
  Pallas kernels  82.3 us (97%)
  local copies, waits for them, and re-layouts  0.97 us (1%)
    pallas_call x1, Pallas kernels, shards(): return lax.switch(which[0], branches, turned, packed)  74.6 us
    pallas_call x1, Pallas kernels, shards(): pl.pallas_call(compact, out_shape=(jax.ShapeDtypeStruct((BLK, TOK), attn_...  7.74 us

profile of v4, /device:TPU:8, one launch (start us, length us, event | category | flops | bytes accessed | tf_op | source)
XLA Modules:
  0.0 84.2 jit_solution(8882215868244327889)
XLA Ops:
  0.0 7.7 %compact.1 = (bf16[128,4096]{1,0:T(8,128)(2,1)S(1)}, bf16[4096,128]{1,0:T(8,128)(2,1)S(1)}, s32[1]{0:T(128)}) custom-call(s32[4]{0:T(128)} %vc_hbm.1, bf16[128,32,128]{2,1,0:T(8,128)(2,1)} %bitcast.3, bf16[128,32,128]{2,1,0:T(8,128)(2,1)} %bitcast.4), custom_call_target="tpu_custom_call" | custom-call | tf_op jit(solution)/shard_map/compact/pallas_call | solution.py:425
  8.4 74.9 %conditional.1 = (f32[256,1024]{1,0:T(8,128)S(1)}) conditional(s32[]{:T(128)} %bitcast.2, (bf16[128,4096]{1,0:T(8,128)(2,1)S(1)}, bf16[4096,128]{1,0:T(8,128)(2,1)S(1)}) %tuple.35, (bf16[128,4096]{1,0:T(8,128)(2,1)S(1)}, bf16[4096,128]{1,0:T(8,128)(2,1)S(1)}) %tuple.35, (bf16[128,4096]{1,0:T(8,128)(2,1)S(1)}, ...), branch_computations={%region_0.0_spmd, %region_1.0_spmd, %region_2.0_spmd, %region_3.0_... | conditional | flops 8589934592 | bytes 3145736 | solution.py:451
  8.4 74.6 %wgrad2944.1 = f32[256,1024]{1,0:T(8,128)S(1)} custom-call(bf16[128,4096]{1,0:T(8,128)(2,1)S(1)} %get-tuple-element.64.a_hbm, bf16[4096,128]{1,0:T(8,128)(2,1)S(1)} %get-tuple-element.65.b_hbm), custom_call_target="tpu_custom_call" | custom-call | flops 6174015488 | bytes 3145728 | tf_op jit(solution)/shard_map/cond/branch_4_fun/wgrad2944/pallas_call | solution.py:451
  83.3 1.0 %copy.25 = f32[256,1024]{1,0:T(8,128)} copy(f32[256,1024]{1,0:T(8,128)S(1)} %get-tuple-element.82) | data formatting | bytes 2097152
